TPU v7x, 512 devices: a whole 4x8x8 slice. The times are simulated.
512 devices in a mesh: bank: 64 (over z, x, core), zero: 8 (over y).
Axes of the slice: x: 4, y: 8, z: 8, core: 2. Of those that a mesh axis runs over, the one named last changes fastest.
Arguments:
- master_down: float32 [64, 1408, 2048], P('bank', None, 'zero'), may hold values from -0.21875 to 0.21875
- second_down: bfloat16 [64, 1408, 2048], P('bank', None, 'zero'), may hold values from -0.078125 to 0.078125
- router_weight: float32 [2048, 64], P('zero', 'bank'), may hold values from -0.125 to 0.125
- router_gain: float32 [2048], P('zero'), may hold values from 0.25 to 1.75
Outputs:
- final_down: bfloat16 [64, 1408, 2048], P('bank')
- scale_down: float32 [64, 1408], P('bank')
- serve_router: bfloat16 [2048, 64], replicated
All inputs are finite; a program needn't handle non-finite values.
Results may differ from a plain program's by a relative error of at most 0.001.
Values may be sent and summed in bfloat16 or wider, within the bound.
A program may use at most 64 MiB of HBM per device.

v0:
```python
import jax
import jax.numpy as jnp
from jax import lax
from jax.sharding import PartitionSpec as P


def from_everyone(value, axis):
    size = lax.axis_size(axis)
    return lax.all_to_all(
        jnp.broadcast_to(value[None], (size, *value.shape)), axis, 0, 0, tiled=True
    )


def over_copies(value, axis):
    return from_everyone(value, axis).sum(axis=0)


def in_order(pieces, dim):
    dims = list(pieces.shape[1:])
    dims[dim] *= pieces.shape[0]
    return jnp.moveaxis(pieces, 0, dim).reshape(dims)


def collect(value, axis, dim):
    return in_order(from_everyone(value, axis), dim)


def body(master_down, second_down, router_weight, router_gain):
    merged_down = master_down + second_down.astype(jnp.float32)
    total_down = over_copies(jnp.sum(merged_down * merged_down, axis=2), "zero")
    scale_down = jnp.sqrt(total_down)
    narrow_down = (merged_down / jnp.expand_dims(scale_down, 2)).astype(jnp.bfloat16)
    final_down = lax.all_gather(narrow_down, "zero", axis=2, tiled=True)
    part_router = (router_weight * router_gain[:, None]).astype(jnp.bfloat16)
    row_router = lax.all_gather(part_router, "zero", axis=0, tiled=True)
    serve_router = collect(row_router, "bank", 1)
    return (final_down, scale_down, serve_router)


def solution(mesh):
    return jax.shard_map(
        body,
        mesh=mesh,
        in_specs=(P("bank", None, "zero"), P("bank", None, "zero"), P("zero", "bank"), P("zero")),
        out_specs=(P("bank", None, None), P("bank", None), P()),
        check_vma=False,
    )
```

profile of v0, /device:TPU:2, one launch (start us, length us, event | category | flops | bytes accessed | tf_op | source)
XLA Modules:
  0.0 115.2 jit_solution(9346307011874724087)
XLA Ops:
  7.2 0.0 copy-start
  7.2 0.0 copy-start.1
  7.2 0.0 all-gather.2.cloned.1.call-start
  7.2 2.0 %multiply_reduce_fusion = f32[1408]{0:T(1024)S(1)} fusion(f32[1,1408,256]{2,1,0:T(8,128)} %param.4, bf16[1,1408,256]{2,1,0:T(8,128)(2,1)} %param.5), kind=kLoop, calls=%fused_computation.1 | loop fusion | flops 1440384 | bytes 2168320 | tf_op jit(solution)/shard_map/reduce_sum | solution.py:30
  9.2 15.1 %all_to_all.10 = f32[8,1,1408]{2,1,0:T(1,128)S(1)} all-to-all(f32[8,1,1408]{2,1,0:T(1,128)S(1)} %broadcast_in_dim.8), channel_id=1, replica_groups=mesh['bank'=64,'zero'=8] {'zero'}, dimensions={0} | all-to-all | bytes 90112 | tf_op jit(solution)/shard_map/all_to_all | solution.py:9
  24.3 0.0 copy-done
  24.4 0.0 copy-done.1
  24.4 0.0 copy-start.2
  24.4 0.0 copy-start.3
  24.4 1.1 divide_convert_fusion
  25.5 0.0 all-gather.2.cloned.1.call-update
  25.5 0.0 copy-done.2
  25.6 13.9 %all_gather.7 = bf16[2048,1]{0,1:T(2,128)(2,1)S(1)} all-gather(bf16[256,1]{0,1:T(2,128)(2,1)S(1)} %multiply_convert_fusion), channel_id=1, replica_groups=mesh['bank'=64,'zero'=8] {'zero'}, dimensions={0}, use_global_device_ids=true | all-gather | bytes 4608 | tf_op jit(solution)/shard_map/all_gather | solution.py:35
  39.5 0.3 broadcast_bitcast_fusion
  39.8 0.5 broadcast.5
  40.3 2.2 %reduce.3 = bf16[64,2048]{1,0:T(8,128)(2,1)S(1)} reduce(bf16[64,1,2048]{2,1,0:T(2,128)(2,1)S(1)} %broadcast_bitcast_fusion, bf16[]{:T(256)} %broadcast.5), dimensions={1}, to_apply=%broadcast_bitcast_fusion.reduce_sub_computation | reduce | bytes 524290
  42.4 0.9 reshape.35
  43.3 14.0 %all-to-all-start.1 = ((bf16[64,2,1024]{2,1,0:T(2,128)(2,1)}), bf16[64,2,1024]{2,1,0:T(2,128)(2,1)S(1)}, u32[]{:S(2)}, u32[]{:S(2)}) async-start(bf16[64,2,1024]{2,1,0:T(2,128)(2,1)} %reshape.35), calls=%async_computation.1 | async-start | bytes 524288 | tf_op jit(solution)/shard_map/all_to_all | solution.py:9
  57.3 0.6 sqrt.19
  57.9 11.6 %all-to-all-done.1 = bf16[64,2,1024]{2,1,0:T(2,128)(2,1)S(1)} async-done(((bf16[64,2,1024]{2,1,0:T(2,128)(2,1)}), bf16[64,2,1024]{2,1,0:T(2,128)(2,1)S(1)}, u32[]{:S(2)}, u32[]{:S(2)}) %all-to-all-start.1) | async-done | bytes 262176 | tf_op jit(solution)/shard_map/all_to_all | solution.py:9
  69.5 0.2 reshape.36
  69.8 0.9 copy.13
  70.6 31.6 %all-gather.2.cloned.1.call-done = bf16[1,1408,2048]{2,1,0:T(8,128)(2,1)} async-done(((bf16[1,1408,256]{2,1,0:T(8,128)(2,1)}), bf16[1,1408,2048]{2,1,0:T(8,128)(2,1)}) %all-gather.2.cloned.1.call-update) | async-done | bytes 5767184 | tf_op jit(solution)/shard_map/all_gather | solution.py:33
  102.2 6.2 %copy.15 = bf16[1,1408,2048]{2,1,0:T(8,128)(2,1)} copy(bf16[1,1408,2048]{2,1,0:T(8,128)(2,1)} %all-gather.2.cloned.1.call-done) | data formatting | bytes 11534336
  (6 shorter events, 0.1 us)
Async XLA Ops:
  7.2 17.2 %copy-start = (f32[1,1408,256]{2,1,0:T(8,128)S(1)}, f32[1,1408,256]{2,1,0:T(8,128)}, u32[]{:S(2)}) copy-start(f32[1,1408,256]{2,1,0:T(8,128)} %param.4) | copy-start | bytes 4325380
  7.2 17.2 %copy-start.1 = (bf16[1,1408,256]{2,1,0:T(8,128)(2,1)S(1)}, bf16[1,1408,256]{2,1,0:T(8,128)(2,1)}, u32[]{:S(2)}) copy-start(bf16[1,1408,256]{2,1,0:T(8,128)(2,1)} %param.5) | copy-start | bytes 2162692
  7.2 95.0 %all-gather.2.cloned.1.call-start = ((), (), s32[]{:S(2)}) async-start(), calls=%async_computation.2 | async-start | bytes 6488064 | tf_op jit(solution)/shard_map/all_gather | solution.py:33
  24.4 1.2 %copy-start.2 = (f32[256,1]{0,1:T(1,128)S(1)}, f32[256,1]{0,1:T(1,128)}, u32[]{:S(2)}) copy-start(f32[256,1]{0,1:T(1,128)} %param.6) | copy-start | bytes 3076
  24.4 1.2 %copy-start.3 = (f32[256]{0:T(256)S(1)}, f32[256]{0:T(256)}, u32[]{:S(2)}) copy-start(f32[256]{0:T(256)} %param.7) | copy-start | bytes 3076
  43.3 26.2 %all-to-all-start.1 = ((bf16[64,2,1024]{2,1,0:T(2,128)(2,1)}), bf16[64,2,1024]{2,1,0:T(2,128)(2,1)S(1)}, u32[]{:S(2)}, u32[]{:S(2)}) async-start(bf16[64,2,1024]{2,1,0:T(2,128)(2,1)} %reshape.35), calls=%async_computation.1 | async-start | bytes 524288 | tf_op jit(solution)/shard_map/all_to_all | solution.py:9
Sparse Core Ops, SparseCore 0:
  25.6 76.5 all-gather.1
where the time goes:
time: 115 us
  waiting for transfers between devices  43.2 us (38%)
  blocking collectives  28.9 us (25%)
  starting transfers between devices  14.1 us (12%)
  between operations  14.1 us (12%)
  local copies, waits for them, and re-layouts  9.55 us (8%)
  other arithmetic  5.32 us (5%)
    all_gather x1, waiting for transfers between devices, body(): final_down = lax.all_gather(narrow_down, 'zero', axis=2, tiled=True)  31.6 us
    all_to_all x1, blocking collectives, from_everyone(): lax.all_to_all(jnp.broadcast_to(value[None], (size, *value.shape)), axis,...  15.1 us
    all_to_all x1, starting transfers between devices, from_everyone(): lax.all_to_all(jnp.broadcast_to(value[None], (size, *value.shape)), axis,...  14 us
    all_gather x1, blocking collectives, body(): row_router = lax.all_gather(part_router, 'zero', axis=0, tiled=True)  13.9 us
    all_to_all x1, waiting for transfers between devices, from_everyone(): lax.all_to_all(jnp.broadcast_to(value[None], (size, *value.shape)), axis,...  11.6 us
    unnamed x13, local copies, waits for them, and re-layouts  8.07 us
  transfers between devices with their start and end apart: 2, of which 2 were waited for; matrix products, arithmetic and copies ran while one was open for 5% of the time, Pallas kernels for 0%

commit v1 on v0

--- a/solution.py
+++ b/solution.py
@@ -30,7 +30,11 @@
     total_down = over_copies(jnp.sum(merged_down * merged_down, axis=2), "zero")
     scale_down = jnp.sqrt(total_down)
     narrow_down = (merged_down / jnp.expand_dims(scale_down, 2)).astype(jnp.bfloat16)
-    final_down = lax.all_gather(narrow_down, "zero", axis=2, tiled=True)
+    size_2 = lax.axis_size("zero")
+    repeats = [size_2 if d == 2 else 1 for d in range(narrow_down.ndim)]
+    final_down = lax.all_to_all(
+        jnp.tile(narrow_down, repeats), "zero", split_axis=2, concat_axis=2, tiled=True
+    )
     part_router = (router_weight * router_gain[:, None]).astype(jnp.bfloat16)
     row_router = lax.all_gather(part_router, "zero", axis=0, tiled=True)
     serve_router = collect(row_router, "bank", 1)

time: 115 us -> 460 us (4.00)
  local copies, waits for them, and re-layouts: 9.55 us -> 158 us
  other arithmetic: 5.32 us -> 129 us
  waiting for transfers between devices: 43.2 us -> 129 us
  between operations: 14.1 us -> 0.77 us
  blocking collectives: 28.9 us -> 16.5 us
  starting transfers between devices: 14.1 us -> 25.8 us
    all_to_all x0 -> x1, waiting for transfers between devices: none -> 129 us  [body(): lax.all_to_all(jnp.tile(narrow_down, repeats), 'zero', split_axis=2, conc...]
    unnamed x1 -> x2, other arithmetic: 2.15 us -> 126 us
    another operation x0 -> x3, local copies, waits for them, and re-layouts: none -> 109 us  [body(): jnp.tile(narrow_down, repeats)]
    unnamed x13 -> x15, local copies, waits for them, and re-layouts: 8.07 us -> 47.2 us
    all_gather x1 -> x0, waiting for transfers between devices: 31.6 us -> none  [body(): final_down = lax.all_gather(narrow_down, 'zero', axis=2, tiled=True)]
    all_to_all x1 -> x0, blocking collectives: 15.1 us -> none  [from_everyone(): lax.all_to_all(jnp.broadcast_to(value[None], (size, *value.shape)), axis,...]
    all_to_all x1 -> x2, waiting for transfers between devices: 11.6 us -> 0.01 us  [from_everyone(): lax.all_to_all(jnp.broadcast_to(value[None], (size, *value.shape)), axis,...]
    all_to_all x1 -> x2, starting transfers between devices: 14 us -> 21.1 us  [from_everyone(): lax.all_to_all(jnp.broadcast_to(value[None], (size, *value.shape)), axis,...]
  transfers between devices with their start and end apart: 2 -> 3, of which waited for: 2 -> 1; matrix products, arithmetic and copies ran while one was open for 5% -> 54% of each run, Pallas kernels for 0% -> 0%
where the time goes in v1:
time: 460 us; the launch traced here: 459 us
  local copies, waits for them, and re-layouts  158 us (34%)
  other arithmetic  129 us (28%)
  waiting for transfers between devices  129 us (28%)
  starting transfers between devices  25.8 us (6%)
  blocking collectives  16.5 us (4%)
    all_to_all x1, waiting for transfers between devices, body(): lax.all_to_all(jnp.tile(narrow_down, repeats), 'zero', split_axis=2, conc...  129 us
    unnamed x2, other arithmetic  126 us
    another operation x3, local copies, waits for them, and re-layouts, body(): jnp.tile(narrow_down, repeats)  109 us
    unnamed x15, local copies, waits for them, and re-layouts  47.2 us
    all_to_all x2, starting transfers between devices, from_everyone(): lax.all_to_all(jnp.broadcast_to(value[None], (size, *value.shape)), axis,...  21.1 us
    all_gather x1, blocking collectives, body(): row_router = lax.all_gather(part_router, 'zero', axis=0, tiled=True)  16.5 us
  transfers between devices with their start and end apart: 3, of which 1 were waited for; matrix products, arithmetic and copies ran while one was open for 54% of the time, Pallas kernels for 0%

profile of v1, /device:TPU:2, one launch (start us, length us, event | category | flops | bytes accessed | tf_op | source)
XLA Modules:
  0.0 458.8 jit_solution(17480194419158915375)
XLA Ops:
  0.7 1.8 multiply_reduce_fusion
  2.5 0.0 copy-start.1
  2.5 0.6 broadcast_in_dim.8
  3.1 7.2 %all-to-all-start = ((f32[8,1,1408]{2,1,0:T(1,128)}), f32[8,1,1408]{2,1,0:T(1,128)S(1)}, u32[]{:S(2)}, u32[]{:S(2)}) async-start(f32[8,1,1408]{2,1,0:T(1,128)} %broadcast_in_dim.8), calls=%async_computation | async-start | bytes 90112 | tf_op jit(solution)/shard_map/all_to_all | solution.py:9
  10.4 16.5 %all_gather.3 = bf16[2048,1]{0,1:T(2,128)(2,1)S(1)} all-gather(bf16[256,1]{0,1:T(2,128)(2,1)S(1)} %multiply_convert_fusion), channel_id=1, replica_groups=mesh['bank'=64,'zero'=8] {'zero'}, dimensions={0}, use_global_device_ids=true | all-gather | bytes 4608 | tf_op jit(solution)/shard_map/all_gather | solution.py:39
  27.0 0.3 broadcast_bitcast_fusion
  27.3 0.5 broadcast.8
  27.8 2.2 reduce.4
  29.9 0.9 reshape.43
  30.8 0.0 all-to-all-done
  30.8 13.9 %all-to-all-start.2 = ((bf16[64,2,1024]{2,1,0:T(2,128)(2,1)}), bf16[64,2,1024]{2,1,0:T(2,128)(2,1)S(1)}, u32[]{:S(2)}, u32[]{:S(2)}) async-start(bf16[64,2,1024]{2,1,0:T(2,128)(2,1)} %reshape.43), calls=%async_computation.2 | async-start | bytes 524288 | tf_op jit(solution)/shard_map/all_to_all | solution.py:9
  44.8 0.3 fusion
  45.1 0.3 copy.18
  45.4 0.4 tile.12
  45.8 108.2 %copy.26 = bf16[1,1408,2048]{1,0,2:T(2,128)(2,1)} copy(bf16[1,1408,2048]{1,2,0:T(8,128)(2,1)S(1)} %bitcast.18) | data formatting | bytes 11534336 | tf_op jit(solution)/shard_map/tile | solution.py:36
  154.0 124.2 %reduce.3 = bf16[2048,1408]{1,0:T(8,128)(2,1)} reduce(bf16[2048,1,1408]{2,1,0:T(2,128)(2,1)} %bitcast.16, bf16[]{:T(256)} %broadcast.8), dimensions={1}, to_apply=%bitcast.15.reduce_sub_computation | reduce | bytes 11534338
  278.2 8.1 %reshape.41 = bf16[8,2,180224]{2,1,0:T(2,128)(2,1)} reshape(bf16[2048,1408]{1,0:T(8,128)(2,1)} %reduce.3) | data formatting | bytes 11534336
  286.3 4.7 %all-to-all-start.1 = ((bf16[8,2,180224]{2,1,0:T(2,128)(2,1)}), bf16[8,2,180224]{2,1,0:T(2,128)(2,1)}, u32[]{:S(2)}, u32[]{:S(2)}) async-start(bf16[8,2,180224]{2,1,0:T(2,128)(2,1)} %reshape.41), calls=%async_computation.1 | async-start | bytes 11534336 | tf_op jit(solution)/shard_map/all_to_all | solution.py:35
  291.0 0.6 sqrt.19
  291.6 0.2 reshape.44
  291.8 0.9 copy.25
  292.7 128.9 %all-to-all-done.1 = bf16[8,2,180224]{2,1,0:T(2,128)(2,1)} async-done(((bf16[8,2,180224]{2,1,0:T(2,128)(2,1)}), bf16[8,2,180224]{2,1,0:T(2,128)(2,1)}, u32[]{:S(2)}, u32[]{:S(2)}) %all-to-all-start.1) | async-done | bytes 5767200 | tf_op jit(solution)/shard_map/all_to_all | solution.py:35
  421.6 10.4 %reshape.42 = bf16[2048,1,1408]{2,1,0:T(2,128)(2,1)} reshape(bf16[8,2,180224]{2,1,0:T(2,128)(2,1)} %all-to-all-done.1) | data formatting | bytes 11534336
  432.0 26.9 %copy.21 = bf16[1,1408,2048]{2,1,0:T(8,128)(2,1)} copy(bf16[1,1408,2048]{1,0,2:T(2,128)(2,1)} %bitcast.17) | data formatting | bytes 11534336
  (12 shorter events, 0.1 us)
Async XLA Ops:
  0.6 9.8 %copy-start.3 = (f32[256]{0:T(256)S(1)}, f32[256]{0:T(256)}, u32[]{:S(2)}) copy-start(f32[256]{0:T(256)} %param.7) | copy-start | bytes 3076
  0.6 9.8 %copy-start.2 = (f32[256,1]{0,1:T(1,128)S(1)}, f32[256,1]{0,1:T(1,128)}, u32[]{:S(2)}) copy-start(f32[256,1]{0,1:T(1,128)} %param.6) | copy-start | bytes 3076
  2.5 42.3 %copy-start = (f32[1,1408,256]{2,1,0:T(8,128)S(1)}, f32[1,1408,256]{2,1,0:T(8,128)}, u32[]{:S(2)}) copy-start(f32[1,1408,256]{2,1,0:T(8,128)} %param.4) | copy-start | bytes 4325380
  2.5 42.3 %copy-start.1 = (bf16[1,1408,256]{2,1,0:T(8,128)(2,1)S(1)}, bf16[1,1408,256]{2,1,0:T(8,128)(2,1)}, u32[]{:S(2)}) copy-start(bf16[1,1408,256]{2,1,0:T(8,128)(2,1)} %param.5) | copy-start | bytes 2162692
  3.1 27.7 %all-to-all-start = ((f32[8,1,1408]{2,1,0:T(1,128)}), f32[8,1,1408]{2,1,0:T(1,128)S(1)}, u32[]{:S(2)}, u32[]{:S(2)}) async-start(f32[8,1,1408]{2,1,0:T(1,128)} %broadcast_in_dim.8), calls=%async_computation | async-start | bytes 90112 | tf_op jit(solution)/shard_map/all_to_all | solution.py:9
  30.8 255.5 %all-to-all-start.2 = ((bf16[64,2,1024]{2,1,0:T(2,128)(2,1)}), bf16[64,2,1024]{2,1,0:T(2,128)(2,1)S(1)}, u32[]{:S(2)}, u32[]{:S(2)}) async-start(bf16[64,2,1024]{2,1,0:T(2,128)(2,1)} %reshape.43), calls=%async_computation.2 | async-start | bytes 524288 | tf_op jit(solution)/shard_map/all_to_all | solution.py:9
  286.3 135.3 %all-to-all-start.1 = ((bf16[8,2,180224]{2,1,0:T(2,128)(2,1)}), bf16[8,2,180224]{2,1,0:T(2,128)(2,1)}, u32[]{:S(2)}, u32[]{:S(2)}) async-start(bf16[8,2,180224]{2,1,0:T(2,128)(2,1)} %reshape.41), calls=%async_computation.1 | async-start | bytes 11534336 | tf_op jit(solution)/shard_map/all_to_all | solution.py:35
